TPU v7x, 32 devices: a whole 2x2x4 slice. The times are simulated.
32 devices in a mesh: pb: 4 (over z), ka: 8 (over y, x, core).
Axes of the slice: x: 2, y: 2, z: 4, core: 2. Of those that a mesh axis runs over, the one named last changes fastest.
Arguments:
- queries: float32 [1, 4096, 128], P(None, ('pb', 'ka')), may hold values from -6 to 6
- keys: float32 [1, 4096, 128], P(None, ('ka', 'pb')), may hold values from -6 to 6
- values: float32 [1, 4096, 128], P(None, ('ka', 'pb')), may hold values from -6 to 6
- tangent_q: float32 [1, 4096, 128], P(None, ('pb', 'ka')), may hold values from -6 to 6
- tangent_k: float32 [1, 4096, 128], P(None, ('ka', 'pb')), may hold values from -6 to 6
- tangent_v: float32 [1, 4096, 128], P(None, ('ka', 'pb')), may hold values from -6 to 6
Outputs:
- attended: float32 [1, 4096, 128], P(None, ('pb', 'ka'))
- attended_tangent: float32 [1, 4096, 128], P(None, ('pb', 'ka'))
All inputs are finite; a program needn't handle non-finite values.
Results may differ from a plain program's by a relative error of at most 0.0003.
Values sent between devices are 32-bit elements; how exact they have to be, the bound alone decides.
No kernel may reach another device: no remote copies, remote signals or barrier semaphores. Data moves between devices by JAX's collectives and lax.ppermute only.
A program may use at most 128 MiB of HBM per device.

v0:
```python
import jax
import jax.numpy as jnp
from jax import lax
from jax.sharding import PartitionSpec as P


def combined_all(value, axis, join):
    pieces = jax.tree.map(lambda part: lax.all_gather(part, axis), value)
    head = jax.tree.map(lambda part: part[0], pieces)
    tail = jax.tree.map(lambda part: part[1:], pieces)
    so_far, _ = lax.scan(lambda so_far, share: (join(so_far, share), None), head, tail)
    return so_far


def join_partials(first, second):
    peak = jnp.maximum(first[0], second[0])
    left = jnp.exp(first[0] - peak)
    right = jnp.exp(second[0] - peak)
    total = first[1] * left + second[1] * right
    numer = first[2] * left[..., None] + second[2] * right[..., None]
    tnumer = first[3] * left[..., None] + second[3] * right[..., None]
    drift = first[4] * left + second[4] * right
    return (peak, total, numer, tnumer, drift)


def body(queries, keys, values, tangent_q, tangent_k, tangent_v):
    highest = lax.Precision.HIGHEST
    head_count, _, width = queries.shape
    factor = width ** (-0.5)
    all_q, all_dq = (
        lax.all_gather(queries, "ka", axis=1, tiled=True),
        lax.all_gather(tangent_q, "ka", axis=1, tiled=True),
    )
    span = all_q.shape[1]
    block = min(512, span)
    blocks = span // block
    split_q = all_q.reshape(head_count, blocks, block, width)
    split_dq = all_dq.reshape(head_count, blocks, block, width)
    start_state = (
        jnp.full((head_count, span), -1e30, jnp.float32),
        jnp.zeros((head_count, span), jnp.float32),
        jnp.zeros((head_count, span, width), jnp.float32),
        jnp.zeros((head_count, span, width), jnp.float32),
        jnp.zeros((head_count, span), jnp.float32),
    )
    piece_k = lax.all_gather(keys, "pb", axis=1, tiled=True)
    piece_dk = lax.all_gather(tangent_k, "pb", axis=1, tiled=True)
    piece_v = lax.all_gather(values, "pb", axis=1, tiled=True)
    piece_dv = lax.all_gather(tangent_v, "pb", axis=1, tiled=True)
    shaped = (
        start_state[0].reshape(head_count, blocks, block),
        start_state[1].reshape(head_count, blocks, block),
        start_state[2].reshape(head_count, blocks, block, width),
        start_state[3].reshape(head_count, blocks, block, width),
        start_state[4].reshape(head_count, blocks, block),
    )

    def one_head(items):
        (
            head_q,
            head_dq,
            head_k,
            head_dk,
            head_v,
            head_dv,
            peak_h,
            total_h,
            numer_h,
            tnumer_h,
            drift_h,
        ) = items

        def one_block(parts):
            query_blk, dquery_blk, old_peak, old_total, old_numer, old_tnumer, old_drift = parts
            scores = jnp.dot(query_blk, head_k.T, precision=highest) * factor
            tangent = (
                jnp.dot(dquery_blk, head_k.T, precision=highest)
                + jnp.dot(query_blk, head_dk.T, precision=highest)
            ) * factor
            new_peak = jnp.maximum(old_peak, jnp.max(scores, axis=1))
            rescale = jnp.exp(old_peak - new_peak)
            weights = jnp.exp(scores - new_peak[:, None])
            product = weights * tangent
            new_total = old_total * rescale + jnp.sum(weights, axis=1)
            new_numer = old_numer * rescale[:, None] + jnp.dot(weights, head_v, precision=highest)
            new_tnumer = (
                old_tnumer * rescale[:, None]
                + jnp.dot(weights, head_dv, precision=highest)
                + jnp.dot(product, head_v, precision=highest)
            )
            new_drift = old_drift * rescale + jnp.sum(product, axis=1)
            return (new_peak, new_total, new_numer, new_tnumer, new_drift)

        return lax.map(one_block, (head_q, head_dq, peak_h, total_h, numer_h, tnumer_h, drift_h))

    result = lax.map(one_head, (split_q, split_dq, piece_k, piece_dk, piece_v, piece_dv) + shaped)
    peak = result[0].reshape(head_count, span)
    total = result[1].reshape(head_count, span)
    numer = result[2].reshape(head_count, span, width)
    tnumer = result[3].reshape(head_count, span, width)
    drift = result[4].reshape(head_count, span)
    merged = combined_all((peak, total, numer, tnumer, drift), "ka", join_partials)
    owned = span // lax.axis_size("ka")
    offset = lax.axis_index("ka") * owned
    total = lax.dynamic_slice_in_dim(merged[1], offset, owned, 1)
    numer = lax.dynamic_slice_in_dim(merged[2], offset, owned, 1)
    tnumer = lax.dynamic_slice_in_dim(merged[3], offset, owned, 1)
    drift = lax.dynamic_slice_in_dim(merged[4], offset, owned, 1)
    attended = numer / total[..., None]
    attended_tangent = tnumer / total[..., None] - attended * (drift / total)[..., None]
    return (attended, attended_tangent)


def solution(mesh):
    return jax.shard_map(
        body,
        mesh=mesh,
        in_specs=(
            P(None, ("pb", "ka"), None),
            P(None, ("ka", "pb"), None),
            P(None, ("ka", "pb"), None),
            P(None, ("pb", "ka"), None),
            P(None, ("ka", "pb"), None),
            P(None, ("ka", "pb"), None),
        ),
        out_specs=(P(None, ("pb", "ka"), None), P(None, ("pb", "ka"), None)),
        check_vma=False,
    )
```

profile of v0, /device:TPU:0, one launch (start us, length us, event | category | flops | bytes accessed | tf_op | source)
XLA Modules:
  0.0 214.0 jit_solution(3527905628978141757)
XLA Ops:
  7.2 0.0 all-gather.5.cloned.1.call-start
  7.3 15.9 %all_gather.34 = f32[1,512,128]{2,1,0:T(8,128)S(1)} all-gather(f32[1,128,128]{2,1,0:T(8,128)} %param.11), channel_id=1, replica_groups=mesh['pb'=4,'ka'=8] {'pb'}, dimensions={1}, use_global_device_ids=true | all-gather | bytes 327680 | tf_op jit(solution)/shard_map/all_gather | solution.py:46
  23.1 14.9 %all_gather.35 = f32[1,512,128]{2,1,0:T(8,128)S(1)} all-gather(f32[1,128,128]{2,1,0:T(8,128)} %param.12), channel_id=1, replica_groups=mesh['pb'=4,'ka'=8] {'pb'}, dimensions={1}, use_global_device_ids=true | all-gather | bytes 327680 | tf_op jit(solution)/shard_map/all_gather | solution.py:48
  38.0 14.0 %all_gather.38 = f32[1,512,128]{2,1,0:T(8,128)S(1)} all-gather(f32[1,128,128]{2,1,0:T(8,128)} %param.14), channel_id=1, replica_groups=mesh['pb'=4,'ka'=8] {'pb'}, dimensions={1}, use_global_device_ids=true | all-gather | bytes 327680 | tf_op jit(solution)/shard_map/all_gather | solution.py:47
  52.1 16.6 %all_gather.36 = f32[1,512,128]{2,1,0:T(8,128)} all-gather(f32[1,128,128]{2,1,0:T(8,128)} %param.15), channel_id=1, replica_groups=mesh['pb'=4,'ka'=8] {'pb'}, dimensions={1}, use_global_device_ids=true | all-gather | bytes 327680 | tf_op jit(solution)/shard_map/all_gather | solution.py:49
  68.6 10.1 %all_gather.33 = f32[1,1024,128]{2,1,0:T(8,128)S(1)} all-gather(f32[1,128,128]{2,1,0:T(8,128)} %param.10), channel_id=1, replica_groups=mesh['pb'=4,'ka'=8] {'ka'}, dimensions={1}, use_global_device_ids=true | all-gather | bytes 589824 | tf_op jit(solution)/shard_map/all_gather | solution.py:31
  78.8 10.8 %all_gather.37 = f32[1,1024,128]{2,1,0:T(8,128)} all-gather(f32[1,128,128]{2,1,0:T(8,128)} %param.13), channel_id=1, replica_groups=mesh['pb'=4,'ka'=8] {'ka'}, dimensions={1}, use_global_device_ids=true | all-gather | bytes 589824 | tf_op jit(solution)/shard_map/all_gather | solution.py:32
  89.5 24.6 %while.53 = (s32[]{:T(128)}, f32[2,512]{1,0:T(2,128)S(1)}, f32[2,512]{1,0:T(2,128)S(1)}, f32[2,512,128]{2,1,0:T(8,128)}, f32[2,512,128]{2,1,0:T(8,128)}, /*index...) while((s32[]{:T(128)}, f32[2,512]{1,0:T(2,128)S(1)}, ...), condition=%wide.region_4.5_spmd, body=%wide.region_0.4_spmd.sunk | while | flops 2419001344 | bytes 12892333 | solution.py:94
  89.5 1.9 fusion.66
  91.5 1.0 fusion.65
  92.5 0.2 fusion.68
  92.7 1.2 fusion.67
  94.0 2.8 %convolution_add_fusion.5 = f32[512,128]{1,0:T(8,128)S(1)} fusion(f32[512,128]{1,0:T(8,128)} %get-tuple-element.549, f32[512,512]{0,1:T(8,128)S(1)} %get-tuple-element.489, f32[512]{0:T(512)S(1)} %get-tuple-element.488, f32[512]{0:T(512)S(1)} %get-tuple-element.492), kind=kOutput, calls=%fused_computation.7.clone.1 | convolution fusion | flops 402980864 | bytes 1576960 | tf_op jit(solution)/shard_map/while/body/eval_jaxpr/while/body/eval_jaxpr/dot_general | solution.py:88
  96.8 2.5 %fusion.71 = f32[2,512,128]{2,1,0:T(8,128)} fusion(f32[2,512,128]{2,1,0:T(8,128)} %get-tuple-element.530, s32[]{:T(128)S(6)} %copy.19, f32[512,128]{1,0:T(8,128)S(1)} %convolution_add_fusion.5, f32[512,512]{0,1:T(8,128)S(1)} %get-tuple-element.493, f32[512,128]{1,0:T(8,128)S(1)} %get-tuple-element.548), kind=kOutput, calls=%fused_computation.6.clone.1 | convolution fusion | flops 402718720 | bytes 1835012 | tf_op jit(solution)/shard_map/while/body/eval_jaxpr/while/body/eval_jaxpr/dot_general | solution.py:89
  99.3 2.5 %fusion.70 = f32[2,512,128]{2,1,0:T(8,128)} fusion(f32[2,512,128]{2,1,0:T(8,128)} %get-tuple-element.529, s32[]{:T(128)S(6)} %copy.19, f32[512,128]{1,0:T(8,128)S(1)} %get-tuple-element.548, f32[512,512]{0,1:T(8,128)S(1)} %get-tuple-element.489, f32[512]{0:T(512)S(1)} %get-tuple-element.488, f32[512]{0:T(512)S(1)} %get-tuple-element.492), kind=kOutput, calls=%fused_computation.10.clone.1 | convolution fusion | flops 402980864 | bytes 1576964 | tf_op jit(solution)/shard_map/while/body/eval_jaxpr/while/body/eval_jaxpr/dot_general | solution.py:85
  101.9 1.9 fusion.66
  103.8 1.0 fusion.65
  104.9 0.2 fusion.68
  105.1 1.2 fusion.67
  106.4 2.8 %convolution_add_fusion.5 = f32[512,128]{1,0:T(8,128)S(1)} fusion(f32[512,128]{1,0:T(8,128)} %get-tuple-element.549, f32[512,512]{0,1:T(8,128)S(1)} %get-tuple-element.489, f32[512]{0:T(512)S(1)} %get-tuple-element.488, f32[512]{0:T(512)S(1)} %get-tuple-element.492), kind=kOutput, calls=%fused_computation.7.clone.1 | convolution fusion | flops 402980864 | bytes 1576960 | tf_op jit(solution)/shard_map/while/body/eval_jaxpr/while/body/eval_jaxpr/dot_general | solution.py:88
  109.1 2.5 %fusion.71 = f32[2,512,128]{2,1,0:T(8,128)} fusion(f32[2,512,128]{2,1,0:T(8,128)} %get-tuple-element.530, s32[]{:T(128)S(6)} %copy.19, f32[512,128]{1,0:T(8,128)S(1)} %convolution_add_fusion.5, f32[512,512]{0,1:T(8,128)S(1)} %get-tuple-element.493, f32[512,128]{1,0:T(8,128)S(1)} %get-tuple-element.548), kind=kOutput, calls=%fused_computation.6.clone.1 | convolution fusion | flops 402718720 | bytes 1835012 | tf_op jit(solution)/shard_map/while/body/eval_jaxpr/while/body/eval_jaxpr/dot_general | solution.py:89
  111.7 2.5 %fusion.70 = f32[2,512,128]{2,1,0:T(8,128)} fusion(f32[2,512,128]{2,1,0:T(8,128)} %get-tuple-element.529, s32[]{:T(128)S(6)} %copy.19, f32[512,128]{1,0:T(8,128)S(1)} %get-tuple-element.548, f32[512,512]{0,1:T(8,128)S(1)} %get-tuple-element.489, f32[512]{0:T(512)S(1)} %get-tuple-element.488, f32[512]{0:T(512)S(1)} %get-tuple-element.492), kind=kOutput, calls=%fused_computation.10.clone.1 | convolution fusion | flops 402980864 | bytes 1576964 | tf_op jit(solution)/shard_map/while/body/eval_jaxpr/while/body/eval_jaxpr/dot_general | solution.py:85
  114.2 0.0 all-gather.5.cloned.1.call-update
  114.2 0.0 all-gather.3.cloned.1.call-start
  114.3 0.7 all-gather.3.cloned.1.call-update
  115.0 8.8 %all_gather.40 = f32[8,1,1024]{2,1,0:T(1,128)S(1)} all-gather(f32[1,1,1024]{2,1,0:T(1,128)S(1)} %all_gather_reshape.16), channel_id=1, replica_groups=mesh['pb'=4,'ka'=8] {'ka'}, dimensions={0}, use_global_device_ids=true | all-gather | bytes 36864 | tf_op jit(solution)/shard_map/all_gather | solution.py:8
  123.8 0.0 copy-start
  123.8 8.6 %all_gather.39 = f32[8,1,1024]{2,1,0:T(1,128)S(1)} all-gather(f32[1,1,1024]{2,1,0:T(1,128)S(1)} %all_gather_reshape.15), channel_id=1, replica_groups=mesh['pb'=4,'ka'=8] {'ka'}, dimensions={0}, use_global_device_ids=true | all-gather | bytes 36864 | tf_op jit(solution)/shard_map/all_gather | solution.py:8
  132.4 0.0 copy-start.1
  132.4 9.0 %all_gather.43 = f32[8,1,1024]{2,1,0:T(1,128)S(1)} all-gather(f32[1,1,1024]{2,1,0:T(1,128)S(1)} %all_gather_reshape.19), channel_id=1, replica_groups=mesh['pb'=4,'ka'=8] {'ka'}, dimensions={0}, use_global_device_ids=true | all-gather | bytes 36864 | tf_op jit(solution)/shard_map/all_gather | solution.py:8
  141.4 0.0 copy-start.2
  141.4 8.8 %all-gather.5.cloned.1.call-done = f32[8,1,1024,128]{3,2,1,0:T(8,128)} async-done(((f32[1,1,1024,128]{3,2,1,0:T(8,128)}), f32[8,1,1024,128]{3,2,1,0:T(8,128)}) %all-gather.5.cloned.1.call-update) | async-done | bytes 4194320 | tf_op jit(solution)/shard_map/all_gather | solution.py:8
  150.2 4.1 %slice.48 = f32[7,1,1024,128]{3,2,1,0:T(8,128)} slice(f32[8,1,1024,128]{3,2,1,0:T(8,128)} %all-gather.5.cloned.1.call-done), slice={[1:8], [0:1], [0:1024], [0:128]} | slice | bytes 7340032 | tf_op jit(solution)/shard_map/slice | solution.py:10
  154.3 1.1 slice_bitcast_fusion
  155.3 0.0 copy-done
  155.4 0.0 copy-done.1
  155.4 0.0 copy-done.2
  155.4 33.3 %all-gather.3.cloned.1.call-done = f32[8,1,1024,128]{3,2,1,0:T(8,128)} async-done(((f32[1,1,1024,128]{3,2,1,0:T(8,128)}), f32[8,1,1024,128]{3,2,1,0:T(8,128)}) %all-gather.3.cloned.1.call-update) | async-done | bytes 4194320 | tf_op jit(solution)/shard_map/all_gather | solution.py:8
  188.7 0.0 slice-start
  188.7 0.0 slice-start.1
  188.7 0.0 slice-start.2
  188.7 1.1 slice_bitcast_fusion.1
  189.8 4.1 %slice.47 = f32[7,1,1024,128]{3,2,1,0:T(8,128)} slice(f32[8,1,1024,128]{3,2,1,0:T(8,128)} %all-gather.3.cloned.1.call-done), slice={[1:8], [0:1], [0:1024], [0:128]} | slice | bytes 7340032 | tf_op jit(solution)/shard_map/slice | solution.py:10
  193.8 0.0 slice-done
  193.8 0.0 slice-done.1
  193.8 0.0 slice-done.2
  193.8 12.5 %while.54 = (s32[]{:T(128)}, f32[1,1024]{1,0:T(1,128)S(1)}, f32[1,1024]{1,0:T(1,128)S(1)}, f32[1,1024,128]{2,1,0:T(8,128)S(1)}, f32[1,1024,128]{2,1,0:T(8,128)S(...) while((s32[]{:T(128)}, f32[1,1024]{1,0:T(1,128)S(1)}, ...), condition=%wide.region_6.7_spmd, body=%wide.region_5.6_spmd.sunk | while | flops 795650 | bytes 3207305 | solution.py:11
  193.9 1.7 fusion.74
  195.7 1.7 fusion.74
  197.5 1.7 fusion.74
  199.3 1.7 fusion.74
  201.1 1.7 fusion.74
  202.9 1.7 fusion.74
  204.7 1.7 fusion.74
  206.4 0.7 multiply_subtract_fusion
  (36 shorter events, 0.8 us)
Async XLA Ops:
  7.2 143.0 %all-gather.5.cloned.1.call-start = ((), (), s32[]{:S(2)}) async-start(), calls=%async_computation.1 | async-start | bytes 4718592 | tf_op jit(solution)/shard_map/all_gather | solution.py:8
  114.2 74.5 %all-gather.3.cloned.1.call-start = ((), (), s32[]{:S(2)}) async-start(), calls=%async_computation | async-start | bytes 4718592 | tf_op jit(solution)/shard_map/all_gather | solution.py:8
  123.8 31.5 %copy-start = (f32[8,1,1024]{2,1,0:T(1,128)}, f32[8,1,1024]{2,1,0:T(1,128)S(1)}, u32[]{:S(2)}) copy-start(f32[8,1,1024]{2,1,0:T(1,128)S(1)} %all_gather.40) | copy-start | bytes 98308
  132.4 22.9 %copy-start.1 = (f32[8,1,1024]{2,1,0:T(1,128)}, f32[8,1,1024]{2,1,0:T(1,128)S(1)}, u32[]{:S(2)}) copy-start(f32[8,1,1024]{2,1,0:T(1,128)S(1)} %all_gather.39) | copy-start | bytes 98308
  141.4 13.9 %copy-start.2 = (f32[8,1,1024]{2,1,0:T(1,128)}, f32[8,1,1024]{2,1,0:T(1,128)S(1)}, u32[]{:S(2)}) copy-start(f32[8,1,1024]{2,1,0:T(1,128)S(1)} %all_gather.43) | copy-start | bytes 98308
  188.7 5.2 %slice-start = ((f32[8,1,1024]{2,1,0:T(1,128)}), f32[7,1,1024]{2,1,0:T(1,128)S(1)}, s32[]{:S(2)}) async-start(f32[8,1,1024]{2,1,0:T(1,128)} %copy-done), calls=%async_computation.2 | async-start | bytes 57344 | tf_op jit(solution)/shard_map/slice | solution.py:10
  188.7 5.2 %slice-start.1 = ((f32[8,1,1024]{2,1,0:T(1,128)}), f32[7,1,1024]{2,1,0:T(1,128)S(1)}, s32[]{:S(2)}) async-start(f32[8,1,1024]{2,1,0:T(1,128)} %copy-done.1), calls=%async_computation.3 | async-start | bytes 57344 | tf_op jit(solution)/shard_map/slice | solution.py:10
  188.7 5.2 %slice-start.2 = ((f32[8,1,1024]{2,1,0:T(1,128)}), f32[7,1,1024]{2,1,0:T(1,128)S(1)}, s32[]{:S(2)}) async-start(f32[8,1,1024]{2,1,0:T(1,128)} %copy-done.2), calls=%async_computation.4 | async-start | bytes 57344 | tf_op jit(solution)/shard_map/slice | solution.py:10
Sparse Core Ops, SparseCore 0:
  114.3 35.8 all-gather.4
  152.1 36.5 all-gather.2
where the time goes:
time: 215 us; the launch traced here: 214 us
  blocking collectives  109 us (51%)
  waiting for transfers between devices  42.8 us (20%)
  matrix products  23.9 us (11%)
  between operations  14.1 us (7%)
  other arithmetic  13.6 us (6%)
  local copies, waits for them, and re-layouts  10.6 us (5%)
    all_gather x2, waiting for transfers between devices, combined_all(): pieces = jax.tree.map(lambda part: lax.all_gather(part, axis), value)  42.1 us
    all_gather x3, blocking collectives, combined_all(): pieces = jax.tree.map(lambda part: lax.all_gather(part, axis), value)  26.4 us
    all_gather x1, blocking collectives, body(): piece_dv = lax.all_gather(tangent_v, 'pb', axis=1, tiled=True)  16.6 us
    all_gather x1, blocking collectives, body(): piece_k = lax.all_gather(keys, 'pb', axis=1, tiled=True)  15.9 us
    all_gather x1, blocking collectives, body(): piece_v = lax.all_gather(values, 'pb', axis=1, tiled=True)  14.9 us
    all_gather x1, blocking collectives, body(): piece_dk = lax.all_gather(tangent_k, 'pb', axis=1, tiled=True)  14 us
    add x7, other arithmetic, join_partials(): tnumer = first[3] * left[..., None] + second[3] * right[..., None]  11.9 us
    all_gather x1, blocking collectives, body(): lax.all_gather(tangent_q, 'ka', axis=1, tiled=True)  10.8 us
  transfers between devices with their start and end apart: 2, of which 2 were waited for; matrix products, arithmetic and copies ran while one was open for 2% of the time, Pallas kernels for 0%

commit v1 on v0

--- a/solution.py
+++ b/solution.py
@@ -43,8 +43,11 @@
         jnp.zeros((head_count, span, width), jnp.float32),
         jnp.zeros((head_count, span), jnp.float32),
     )
-    piece_k = lax.all_gather(keys, "pb", axis=1, tiled=True)
-    piece_dk = lax.all_gather(tangent_k, "pb", axis=1, tiled=True)
+    piece_k, piece_dk = jnp.split(
+        lax.all_gather(jnp.concatenate([keys, tangent_k], axis=0), "pb", axis=1, tiled=True),
+        [keys.shape[0]],
+        axis=0,
+    )
     piece_v = lax.all_gather(values, "pb", axis=1, tiled=True)
     piece_dv = lax.all_gather(tangent_v, "pb", axis=1, tiled=True)
     shaped = (

time: 215 us -> 202 us (0.940)
  blocking collectives: 109 us -> 94.7 us
    all_gather x2 -> x1, blocking collectives: 29.9 us -> 14.9 us  [body(): lax.all_gather(jnp.concatenate([keys, tangent_k], axis=0), 'pb', axis=1,...]
  transfers between devices with their start and end apart: 2 -> 2, of which waited for: 2 -> 2; matrix products, arithmetic and copies ran while one was open for 2% -> 3% of each run, Pallas kernels for 0% -> 0%
where the time goes in v1:
time: 202 us; the launch traced here: 201 us
  blocking collectives  94.7 us (47%)
  waiting for transfers between devices  43.1 us (21%)
  matrix products  23.9 us (12%)
  other arithmetic  14.4 us (7%)
  between operations  14.1 us (7%)
  local copies, waits for them, and re-layouts  10.7 us (5%)
    all_gather x2, waiting for transfers between devices, combined_all(): pieces = jax.tree.map(lambda part: lax.all_gather(part, axis), value)  42.4 us
    all_gather x3, blocking collectives, combined_all(): pieces = jax.tree.map(lambda part: lax.all_gather(part, axis), value)  26.4 us
    all_gather x1, blocking collectives, body(): piece_dv = lax.all_gather(tangent_v, 'pb', axis=1, tiled=True)  16.6 us
    all_gather x1, blocking collectives, body(): piece_v = lax.all_gather(values, 'pb', axis=1, tiled=True)  15.9 us
    all_gather x1, blocking collectives, body(): lax.all_gather(jnp.concatenate([keys, tangent_k], axis=0), 'pb', axis=1,...  14.9 us
    add x7, other arithmetic, join_partials(): tnumer = first[3] * left[..., None] + second[3] * right[..., None]  11.9 us
    all_gather x1, blocking collectives, body(): lax.all_gather(tangent_q, 'ka', axis=1, tiled=True)  10.8 us
    all_gather x1, blocking collectives, body(): lax.all_gather(queries, 'ka', axis=1, tiled=True)  10.2 us
  transfers between devices with their start and end apart: 2, of which 2 were waited for; matrix products, arithmetic and copies ran while one was open for 3% of the time, Pallas kernels for 0%

profile of v1, /device:TPU:0, one launch (start us, length us, event | category | flops | bytes accessed | tf_op | source)
XLA Modules:
  0.0 201.2 jit_solution(11854006720202683521)
XLA Ops:
  7.2 0.0 all-gather.5.cloned.1.call-start
  7.3 15.9 %all_gather.32 = f32[1,512,128]{2,1,0:T(8,128)S(1)} all-gather(f32[1,128,128]{2,1,0:T(8,128)} %param.12), channel_id=1, replica_groups=mesh['pb'=4,'ka'=8] {'pb'}, dimensions={1}, use_global_device_ids=true | all-gather | bytes 327680 | tf_op jit(solution)/shard_map/all_gather | solution.py:51
  23.1 16.6 %all_gather.33 = f32[1,512,128]{2,1,0:T(8,128)} all-gather(f32[1,128,128]{2,1,0:T(8,128)} %param.15), channel_id=1, replica_groups=mesh['pb'=4,'ka'=8] {'pb'}, dimensions={1}, use_global_device_ids=true | all-gather | bytes 327680 | tf_op jit(solution)/shard_map/all_gather | solution.py:52
  39.7 0.9 pad_maximum_fusion
  40.6 14.9 %all_gather.31 = f32[2,512,128]{2,1,0:T(8,128)S(1)} all-gather(f32[2,128,128]{2,1,0:T(8,128)S(1)} %pad_maximum_fusion), channel_id=1, replica_groups=mesh['pb'=4,'ka'=8] {'pb'}, dimensions={1}, use_global_device_ids=true | all-gather | bytes 655360 | tf_op jit(solution)/shard_map/all_gather | solution.py:47
  55.5 10.2 %all_gather.30 = f32[1,1024,128]{2,1,0:T(8,128)S(1)} all-gather(f32[1,128,128]{2,1,0:T(8,128)} %param.10), channel_id=1, replica_groups=mesh['pb'=4,'ka'=8] {'ka'}, dimensions={1}, use_global_device_ids=true | all-gather | bytes 589824 | tf_op jit(solution)/shard_map/all_gather | solution.py:31
  65.7 10.8 %all_gather.34 = f32[1,1024,128]{2,1,0:T(8,128)} all-gather(f32[1,128,128]{2,1,0:T(8,128)} %param.13), channel_id=1, replica_groups=mesh['pb'=4,'ka'=8] {'ka'}, dimensions={1}, use_global_device_ids=true | all-gather | bytes 589824 | tf_op jit(solution)/shard_map/all_gather | solution.py:32
  76.5 24.6 %while.53 = (s32[]{:T(128)}, f32[2,512]{1,0:T(2,128)S(1)}, f32[2,512]{1,0:T(2,128)S(1)}, f32[2,512,128]{2,1,0:T(8,128)}, f32[2,512,128]{2,1,0:T(8,128)}, /*index...) while((s32[]{:T(128)}, f32[2,512]{1,0:T(2,128)S(1)}, ...), condition=%wide.region_4.5_spmd, body=%wide.region_0.4_spmd.sunk | while | flops 2419001344 | bytes 12892333 | solution.py:97
  76.5 1.9 fusion.66
  78.4 1.0 fusion.65
  79.4 0.2 fusion.68
  79.6 1.2 fusion.67
  80.9 2.8 %convolution_add_fusion.5 = f32[512,128]{1,0:T(8,128)S(1)} fusion(f32[512,128]{1,0:T(8,128)} %get-tuple-element.551, f32[512,512]{0,1:T(8,128)S(1)} %get-tuple-element.491, f32[512]{0:T(512)S(1)} %get-tuple-element.490, f32[512]{0:T(512)S(1)} %get-tuple-element.494), kind=kOutput, calls=%fused_computation.7.clone.1 | convolution fusion | flops 402980864 | bytes 1576960 | tf_op jit(solution)/shard_map/while/body/eval_jaxpr/while/body/eval_jaxpr/dot_general | solution.py:91
  83.7 2.5 %fusion.71 = f32[2,512,128]{2,1,0:T(8,128)} fusion(f32[2,512,128]{2,1,0:T(8,128)} %get-tuple-element.532, s32[]{:T(128)S(6)} %copy.19, f32[512,128]{1,0:T(8,128)S(1)} %convolution_add_fusion.5, f32[512,512]{0,1:T(8,128)S(1)} %get-tuple-element.495, f32[512,128]{1,0:T(8,128)S(1)} %get-tuple-element.550), kind=kOutput, calls=%fused_computation.6.clone.1 | convolution fusion | flops 402718720 | bytes 1835012 | tf_op jit(solution)/shard_map/while/body/eval_jaxpr/while/body/eval_jaxpr/dot_general | solution.py:92
  86.2 2.5 %fusion.70 = f32[2,512,128]{2,1,0:T(8,128)} fusion(f32[2,512,128]{2,1,0:T(8,128)} %get-tuple-element.531, s32[]{:T(128)S(6)} %copy.19, f32[512,128]{1,0:T(8,128)S(1)} %get-tuple-element.550, f32[512,512]{0,1:T(8,128)S(1)} %get-tuple-element.491, f32[512]{0:T(512)S(1)} %get-tuple-element.490, f32[512]{0:T(512)S(1)} %get-tuple-element.494), kind=kOutput, calls=%fused_computation.10.clone.1 | convolution fusion | flops 402980864 | bytes 1576964 | tf_op jit(solution)/shard_map/while/body/eval_jaxpr/while/body/eval_jaxpr/dot_general | solution.py:88
  88.8 1.9 fusion.66
  90.7 1.0 fusion.65
  91.7 0.2 fusion.68
  91.9 1.2 fusion.67
  93.2 2.8 %convolution_add_fusion.5 = f32[512,128]{1,0:T(8,128)S(1)} fusion(f32[512,128]{1,0:T(8,128)} %get-tuple-element.551, f32[512,512]{0,1:T(8,128)S(1)} %get-tuple-element.491, f32[512]{0:T(512)S(1)} %get-tuple-element.490, f32[512]{0:T(512)S(1)} %get-tuple-element.494), kind=kOutput, calls=%fused_computation.7.clone.1 | convolution fusion | flops 402980864 | bytes 1576960 | tf_op jit(solution)/shard_map/while/body/eval_jaxpr/while/body/eval_jaxpr/dot_general | solution.py:91
  96.0 2.5 %fusion.71 = f32[2,512,128]{2,1,0:T(8,128)} fusion(f32[2,512,128]{2,1,0:T(8,128)} %get-tuple-element.532, s32[]{:T(128)S(6)} %copy.19, f32[512,128]{1,0:T(8,128)S(1)} %convolution_add_fusion.5, f32[512,512]{0,1:T(8,128)S(1)} %get-tuple-element.495, f32[512,128]{1,0:T(8,128)S(1)} %get-tuple-element.550), kind=kOutput, calls=%fused_computation.6.clone.1 | convolution fusion | flops 402718720 | bytes 1835012 | tf_op jit(solution)/shard_map/while/body/eval_jaxpr/while/body/eval_jaxpr/dot_general | solution.py:92
  98.6 2.5 %fusion.70 = f32[2,512,128]{2,1,0:T(8,128)} fusion(f32[2,512,128]{2,1,0:T(8,128)} %get-tuple-element.531, s32[]{:T(128)S(6)} %copy.19, f32[512,128]{1,0:T(8,128)S(1)} %get-tuple-element.550, f32[512,512]{0,1:T(8,128)S(1)} %get-tuple-element.491, f32[512]{0:T(512)S(1)} %get-tuple-element.490, f32[512]{0:T(512)S(1)} %get-tuple-element.494), kind=kOutput, calls=%fused_computation.10.clone.1 | convolution fusion | flops 402980864 | bytes 1576964 | tf_op jit(solution)/shard_map/while/body/eval_jaxpr/while/body/eval_jaxpr/dot_general | solution.py:88
  101.1 0.0 all-gather.5.cloned.1.call-update
  101.1 0.0 all-gather.3.cloned.1.call-start
  101.2 0.7 all-gather.3.cloned.1.call-update
  101.9 8.8 %all_gather.36 = f32[8,1,1024]{2,1,0:T(1,128)S(1)} all-gather(f32[1,1,1024]{2,1,0:T(1,128)S(1)} %all_gather_reshape.16), channel_id=1, replica_groups=mesh['pb'=4,'ka'=8] {'ka'}, dimensions={0}, use_global_device_ids=true | all-gather | bytes 36864 | tf_op jit(solution)/shard_map/all_gather | solution.py:8
  110.7 0.0 copy-start
  110.7 8.6 %all_gather.35 = f32[8,1,1024]{2,1,0:T(1,128)S(1)} all-gather(f32[1,1,1024]{2,1,0:T(1,128)S(1)} %all_gather_reshape.15), channel_id=1, replica_groups=mesh['pb'=4,'ka'=8] {'ka'}, dimensions={0}, use_global_device_ids=true | all-gather | bytes 36864 | tf_op jit(solution)/shard_map/all_gather | solution.py:8
  119.3 0.0 copy-start.1
  119.3 9.0 %all_gather.39 = f32[8,1,1024]{2,1,0:T(1,128)S(1)} all-gather(f32[1,1,1024]{2,1,0:T(1,128)S(1)} %all_gather_reshape.19), channel_id=1, replica_groups=mesh['pb'=4,'ka'=8] {'ka'}, dimensions={0}, use_global_device_ids=true | all-gather | bytes 36864 | tf_op jit(solution)/shard_map/all_gather | solution.py:8
  128.3 0.0 copy-start.2
  128.3 9.1 %all-gather.5.cloned.1.call-done = f32[8,1,1024,128]{3,2,1,0:T(8,128)} async-done(((f32[1,1,1024,128]{3,2,1,0:T(8,128)}), f32[8,1,1024,128]{3,2,1,0:T(8,128)}) %all-gather.5.cloned.1.call-update) | async-done | bytes 4194320 | tf_op jit(solution)/shard_map/all_gather | solution.py:8
  137.4 4.1 %slice.48 = f32[7,1,1024,128]{3,2,1,0:T(8,128)} slice(f32[8,1,1024,128]{3,2,1,0:T(8,128)} %all-gather.5.cloned.1.call-done), slice={[1:8], [0:1], [0:1024], [0:128]} | slice | bytes 7340032 | tf_op jit(solution)/shard_map/slice | solution.py:10
  141.4 1.1 slice_bitcast_fusion
  142.5 0.0 copy-done
  142.5 0.0 copy-done.1
  142.5 0.0 copy-done.2
  142.5 33.3 %all-gather.3.cloned.1.call-done = f32[8,1,1024,128]{3,2,1,0:T(8,128)} async-done(((f32[1,1,1024,128]{3,2,1,0:T(8,128)}), f32[8,1,1024,128]{3,2,1,0:T(8,128)}) %all-gather.3.cloned.1.call-update) | async-done | bytes 4194320 | tf_op jit(solution)/shard_map/all_gather | solution.py:8
  175.9 0.0 slice-start
  175.9 0.0 slice-start.1
  175.9 0.0 slice-start.2
  175.9 1.1 slice_bitcast_fusion.1
  177.0 4.1 %slice.47 = f32[7,1,1024,128]{3,2,1,0:T(8,128)} slice(f32[8,1,1024,128]{3,2,1,0:T(8,128)} %all-gather.3.cloned.1.call-done), slice={[1:8], [0:1], [0:1024], [0:128]} | slice | bytes 7340032 | tf_op jit(solution)/shard_map/slice | solution.py:10
  181.0 0.0 slice-done
  181.0 0.0 slice-done.1
  181.0 0.0 slice-done.2
  181.0 12.5 %while.54 = (s32[]{:T(128)}, f32[1,1024]{1,0:T(1,128)S(1)}, f32[1,1024]{1,0:T(1,128)S(1)}, f32[1,1024,128]{2,1,0:T(8,128)S(1)}, f32[1,1024,128]{2,1,0:T(8,128)S(...) while((s32[]{:T(128)}, f32[1,1024]{1,0:T(1,128)S(1)}, ...), condition=%wide.region_6.7_spmd, body=%wide.region_5.6_spmd.sunk | while | flops 795650 | bytes 3207305 | solution.py:11
  181.1 1.7 fusion.74
  182.9 1.7 fusion.74
  184.7 1.7 fusion.74
  186.5 1.7 fusion.74
  188.3 1.7 fusion.74
  190.0 1.7 fusion.74
  191.8 1.7 fusion.74
  193.6 0.7 multiply_subtract_fusion
  (37 shorter events, 0.8 us)
Async XLA Ops:
  7.2 130.2 %all-gather.5.cloned.1.call-start = ((), (), s32[]{:S(2)}) async-start(), calls=%async_computation.1 | async-start | bytes 4718592 | tf_op jit(solution)/shard_map/all_gather | solution.py:8
  101.1 74.8 %all-gather.3.cloned.1.call-start = ((), (), s32[]{:S(2)}) async-start(), calls=%async_computation | async-start | bytes 4718592 | tf_op jit(solution)/shard_map/all_gather | solution.py:8
  110.7 31.8 %copy-start = (f32[8,1,1024]{2,1,0:T(1,128)}, f32[8,1,1024]{2,1,0:T(1,128)S(1)}, u32[]{:S(2)}) copy-start(f32[8,1,1024]{2,1,0:T(1,128)S(1)} %all_gather.36) | copy-start | bytes 98308
  119.3 23.2 %copy-start.1 = (f32[8,1,1024]{2,1,0:T(1,128)}, f32[8,1,1024]{2,1,0:T(1,128)S(1)}, u32[]{:S(2)}) copy-start(f32[8,1,1024]{2,1,0:T(1,128)S(1)} %all_gather.35) | copy-start | bytes 98308
  128.3 14.2 %copy-start.2 = (f32[8,1,1024]{2,1,0:T(1,128)}, f32[8,1,1024]{2,1,0:T(1,128)S(1)}, u32[]{:S(2)}) copy-start(f32[8,1,1024]{2,1,0:T(1,128)S(1)} %all_gather.39) | copy-start | bytes 98308
  175.9 5.2 %slice-start = ((f32[8,1,1024]{2,1,0:T(1,128)}), f32[7,1,1024]{2,1,0:T(1,128)S(1)}, s32[]{:S(2)}) async-start(f32[8,1,1024]{2,1,0:T(1,128)} %copy-done), calls=%async_computation.2 | async-start | bytes 57344 | tf_op jit(solution)/shard_map/slice | solution.py:10
  175.9 5.2 %slice-start.1 = ((f32[8,1,1024]{2,1,0:T(1,128)}), f32[7,1,1024]{2,1,0:T(1,128)S(1)}, s32[]{:S(2)}) async-start(f32[8,1,1024]{2,1,0:T(1,128)} %copy-done.1), calls=%async_computation.3 | async-start | bytes 57344 | tf_op jit(solution)/shard_map/slice | solution.py:10
  175.9 5.2 %slice-start.2 = ((f32[8,1,1024]{2,1,0:T(1,128)}), f32[7,1,1024]{2,1,0:T(1,128)S(1)}, s32[]{:S(2)}) async-start(f32[8,1,1024]{2,1,0:T(1,128)} %copy-done.2), calls=%async_computation.4 | async-start | bytes 57344 | tf_op jit(solution)/shard_map/slice | solution.py:10
Sparse Core Ops, SparseCore 0:
  101.2 36.0 all-gather.4
  139.2 36.5 all-gather.2
